TPU v7x, 32 devices: a whole 2x2x4 slice. The times are simulated.
32 devices in a mesh: atoms: 8 (over z, y), modes: 4 (over x, core).
Axes of the slice: x: 2, y: 2, z: 4, core: 2. Of those that a mesh axis runs over, the one named last changes fastest.
Arguments:
- eigvec: bfloat16 [3072, 2048], P('atoms', 'modes'), may hold values from -6 to 6
- operator_blocks: bfloat16 [24, 8, 128, 128], P('atoms'), may hold values from -0.0034179688 to 0.0034179688
- column_blocks: int32 [24, 8], P('atoms'), may hold values from 0 to 23, as said below
- block_mask: int32 [24, 8], P('atoms'), may hold values 0 or 1
- spectrum: float32 [3072], replicated, may hold values from 0.5 to 20
- mode_index: int32 [2048], replicated, may hold values from 0 to 3071
- linewidth: float32 [2048], replicated, may hold values from 0.05 to 1
Outputs:
- flux_tiles: float32 [2048, 2048], P('modes', 'atoms')
- diffusivity: float32 [2048], P('modes')
Inputs may be any that keep to these rules, and one draw needn't show every extreme that they name: `column_blocks`: the 8 column blocks of row block r are distinct and lie within 4 blocks of r, counted around the cycle of 24 blocks.
All inputs are finite; a program needn't handle non-finite values. No bound on the sum of `block_mask` on one device may be relied on, other than what follows from the above.
Results may differ from a plain program's by a relative error of at most 0.0058.
Values may be sent and summed in bfloat16 or wider, within the bound.
No kernel may reach another device: no remote copies, remote signals or barrier semaphores. Data moves between devices by JAX's collectives and lax.ppermute only.
A program may use at most 64 MiB of HBM per device.

v0:
```python
import jax
import jax.numpy as jnp
from jax import lax
from jax.sharding import PartitionSpec as P

REACH = 4


def with_halo(block, sides, width):
    for axis, dim in sides:
        count = lax.axis_size(axis)
        forward = [(i, i + 1) for i in range(count - 1)]
        forward.append((count - 1, 0))
        backward = [(target, source) for source, target in forward]
        low = lax.ppermute(
            lax.slice_in_dim(block, block.shape[dim] - width, None, axis=dim), axis, forward
        )
        high = lax.ppermute(lax.slice_in_dim(block, 0, width, axis=dim), axis, backward)
        block = jnp.concatenate([low, block, high], axis=dim)
    return block


def from_behind(value, axis, by):
    devices = lax.axis_size(axis)
    return lax.ppermute(value, axis, [(i, (i + by) % devices) for i in range(devices)])


def pair_weight(row_freq, col_freq, row_width, col_width):
    freq_sum = row_freq[:, None] + col_freq[None, :]
    spacing = row_freq[:, None] - col_freq[None, :]
    mean_width = 0.5 * (row_width[:, None] + col_width[None, :])
    factor = freq_sum * freq_sum / (4.0 * row_freq[:, None] * col_freq[None, :])
    return factor * mean_width / (spacing * spacing + mean_width * mean_width)


def body(eigvec, operator_blocks, column_blocks, block_mask, spectrum, mode_index, linewidth):
    block_width = operator_blocks.shape[2]
    local_blocks = operator_blocks.shape[0]
    own_modes = eigvec.shape[1]
    atom_count = lax.axis_size("atoms")
    atom_rank = lax.axis_index("atoms")
    group_rank = lax.axis_index("modes")
    total_blocks = local_blocks * atom_count
    near_blocks = min(REACH, local_blocks)
    extra_blocks = REACH - near_blocks
    extended = with_halo(eigvec, (("atoms", 0),), near_blocks * block_width)
    far_pieces = []
    slab_rows = eigvec.shape[0]
    for distance, far_rows in (
        (2, eigvec[slab_rows - extra_blocks * block_width :]),
        (-2, eigvec[: extra_blocks * block_width]),
    ):
        far_pieces.append(from_behind(far_rows, "atoms", distance))
    extended = jnp.concatenate([far_pieces[0], extended, far_pieces[1]], axis=0)
    ext_blocks = extended.reshape(-1, block_width, own_modes)
    offsets = (column_blocks - atom_rank * local_blocks + REACH) % total_blocks
    picked = ext_blocks[offsets]
    masked = jnp.where(
        block_mask[:, :, None, None] > 0, operator_blocks, jnp.zeros((), operator_blocks.dtype)
    )
    product = jnp.einsum("bsij,bsjm->bim", masked, picked, preferred_element_type=jnp.float32)
    velocity = product.reshape(-1, own_modes).astype(jnp.bfloat16)
    contract = (((0,), (0,)), ((), ()))
    stacked = jnp.stack((eigvec, velocity))
    piece = lax.all_gather(stacked, "modes", axis=2, tiled=True)
    direct = lax.dot_general(eigvec, piece[1], contract, preferred_element_type=jnp.float32)
    mirror = lax.dot_general(velocity, piece[0], contract, preferred_element_type=jnp.float32)
    partial_flux = direct - mirror
    frequency = spectrum[mode_index]
    mode_total = frequency.shape[0]
    row_freq = lax.dynamic_slice_in_dim(frequency, group_rank * own_modes, own_modes)
    row_width = lax.dynamic_slice_in_dim(linewidth, group_rank * own_modes, own_modes)
    flux_tiles = lax.psum_scatter(partial_flux, "atoms", scatter_dimension=1, tiled=True)
    share_cols = flux_tiles.shape[1]
    col_freq = lax.dynamic_slice_in_dim(frequency, atom_rank * share_cols, share_cols)
    col_width = lax.dynamic_slice_in_dim(linewidth, atom_rank * share_cols, share_cols)
    weight = pair_weight(row_freq, col_freq, row_width, col_width)
    partial_sums = jnp.sum(weight * flux_tiles * flux_tiles, axis=1)
    diffusivity = lax.psum(partial_sums, "atoms") / mode_total
    return (flux_tiles, diffusivity)


def solution(mesh):
    return jax.shard_map(
        body,
        mesh=mesh,
        in_specs=(
            P("atoms", "modes"),
            P("atoms", None, None, None),
            P("atoms", None),
            P("atoms", None),
            P(),
            P(),
            P(),
        ),
        out_specs=(P("modes", "atoms"), P("modes")),
        check_vma=False,
    )
```

profile of v0, /device:TPU:0, one launch (start us, length us, event | category | flops | bytes accessed | tf_op | source)
XLA Modules:
  0.0 190.7 jit_solution(3013276178611091838)
XLA Ops:
  7.2 0.0 copy-start
  7.2 0.0 copy-start.2
  7.2 0.0 all-gather.2.cloned.1.call-start
  7.2 3.0 %collective-permute-start.1 = (bf16[384,512]{1,0:T(8,128)(2,1)}, bf16[384,512]{1,0:T(8,128)(2,1)S(1)}, u32[]{:S(2)}, u32[]{:S(2)}) collective-permute-start(bf16[384,512]{1,0:T(8,128)(2,1)} %param.7), channel_id=1, source_target_pairs={{0,4},{4,8},{8,12},{12,16},{16,20},{20,24},{24,28},{28,0},{1,5},{5... | collective-permute-start | bytes 1179656 | tf_op jit(solution)/shard_map/ppermute | solution.py:15
  10.3 3.1 %collective-permute-start.2 = (bf16[384,512]{1,0:T(8,128)(2,1)}, bf16[384,512]{1,0:T(8,128)(2,1)S(1)}, u32[]{:S(2)}, u32[]{:S(2)}) collective-permute-start(bf16[384,512]{1,0:T(8,128)(2,1)} %param.7), channel_id=1, source_target_pairs={{4,0},{8,4},{12,8},{16,12},{20,16},{24,20},{28,24},{0,28},{5,1},{9... | collective-permute-start | bytes 1179656 | tf_op jit(solution)/shard_map/ppermute | solution.py:18
  13.4 1.0 fusion.8
  14.4 0.1 collective-permute-start
  14.4 3.8 %collective-permute-start.3 = (bf16[128,512]{1,0:T(8,128)(2,1)S(1)}, bf16[128,512]{1,0:T(8,128)(2,1)S(1)}, u32[]{:S(2)}, u32[]{:S(2)}) collective-permute-start(bf16[128,512]{1,0:T(8,128)(2,1)S(1)} %get-tuple-element.8), channel_id=1, source_target_pairs={{0,24},{4,28},{8,0},{12,4},{16,8},{20,12},{24,16},{28,20},{1,25},{... | collective-permute-start | bytes 393224 | tf_op jit(solution)/shard_map/ppermute | solution.py:25
  18.3 0.7 compare_select_fusion.1
  19.0 1.2 broadcast_compare_fusion
  20.2 0.1 reshape.31
  20.2 8.0 %collective-permute-done = bf16[128,512]{1,0:T(8,128)(2,1)S(1)} collective-permute-done((bf16[128,512]{1,0:T(8,128)(2,1)S(1)}, bf16[128,512]{1,0:T(8,128)(2,1)S(1)}, u32[]{:S(2)}, u32[]{:S(2)}) %collective-permute-start) | collective-permute-done | bytes 131104 | tf_op jit(solution)/shard_map/ppermute | solution.py:25
  28.3 0.0 collective-permute-done.1
  28.3 0.0 copy-done.2
  28.4 1.1 collective-permute-done.2
  29.5 0.0 collective-permute-done.3
  29.6 0.0 copy-start.1
  29.6 1.1 copy-done.1
  30.7 2.1 %gather_fusion = bf16[24,128,512]{2,1,0:T(8,128)(2,1)S(1)} fusion(bf16[11,128,512]{2,1,0:T(8,128)(2,1)} %bitcast.22, s32[1024]{0:T(1024)S(1)} %pad_clamp_fusion), kind=kCustom, calls=%fused_computation | custom fusion | bytes 6291552 | tf_op jit(solution)/shard_map/gather | solution.py:57
  32.8 1.8 fusion.1
  34.6 0.0 copy-start.4
  34.6 0.7 copy-done.4
  35.3 1.0 pad_maximum_fusion
  36.3 0.0 all-gather.2.cloned.1.call-update
  36.3 0.0 copy-start.5
  36.3 0.0 reduce-scatter.2.cloned.1.call-start
  36.4 28.7 %all-gather.2.cloned.1.call-done = bf16[2,384,2048]{2,1,0:T(8,128)(2,1)} async-done(((bf16[2,384,512]{2,1,0:T(8,128)(2,1)}), bf16[2,384,2048]{2,1,0:T(8,128)(2,1)}) %all-gather.2.cloned.1.call-update) | async-done | bytes 3145744 | tf_op jit(solution)/shard_map/all_gather | solution.py:65
  65.1 0.0 copy-start.3
  65.1 2.9 %fusion = f32[2048,512]{1,0:T(8,128)S(1)} fusion(bf16[384,512]{1,0:T(8,128)(2,1)S(1)} %copy-done.2, bf16[2,384,2048]{2,1,0:T(8,128)(2,1)} %all-gather.2.cloned.1.call-done), kind=kOutput, calls=%fused_computation.5 | convolution fusion | flops 805306368 | bytes 6160384 | tf_op jit(solution)/shard_map/dot_general | solution.py:66
  68.0 0.0 copy-done.5
  68.0 0.0 copy-done.3
  68.0 3.3 %bitcast_subtract_fusion = f32[512,2048]{0,1:T(8,128)} fusion(f32[2048,512]{1,0:T(8,128)S(1)} %fusion, bf16[384,512]{1,0:T(8,128)(2,1)S(1)} %bitcast.25, bf16[2,384,2048]{2,1,0:T(8,128)(2,1)S(1)} %copy-done.3), kind=kOutput, calls=%fused_computation.2 | convolution fusion | flops 806354944 | bytes 10354688 | tf_op jit(solution)/shard_map/dot_general | solution.py:67
  71.2 0.0 copy-start.6
  71.2 0.0 reduce-scatter.2.cloned.1.call-update
  71.3 0.7 copy-done.6
  71.9 0.0 copy-done
  71.9 11.8 %gather_fusion.1 = f32[2048]{0:T(1024)S(1)} fusion(f32[3072]{0:T(1024)S(1)} %copy-done, s32[2048]{0:T(1024)S(1)} %fusion.6), kind=kCustom, calls=%fused_computation.1 | custom fusion | bytes 24576 | tf_op jit(solution)/shard_map/gather | solution.py:69
  83.7 0.1 dynamic_slice.13
  83.8 0.8 dynamic_slice.15
  84.6 0.8 dynamic_slice.14
  85.3 0.1 broadcast_multiply_fusion.1
  85.4 74.3 %reduce-scatter.2.cloned.1.call-done = f32[512,256]{0,1:T(8,128)} async-done(((f32[512,2048]{0,1:T(8,128)}), f32[512,256]{0,1:T(8,128)}) %reduce-scatter.2.cloned.1.call-update) | async-done | bytes 524304 | tf_op jit(solution)/shard_map/reduce_scatter | solution.py:73
  159.7 1.4 fusion.4
  161.2 20.1 %psum.7 = f32[512]{0:T(512)S(1)} all-reduce(f32[512]{0:T(512)S(1)} %fusion.4), channel_id=1, replica_groups=mesh['atoms'=8,'modes'=4] {'atoms'}, use_global_device_ids=true, to_apply=%region_2.3 | all-reduce | flops 512 | bytes 4096 | tf_op jit(solution)/shard_map/psum | solution.py:79
  181.2 0.6 broadcast_multiply_fusion
  181.8 2.0 %copy.12 = f32[512,256]{1,0:T(8,128)} copy(f32[512,256]{0,1:T(8,128)} %reduce-scatter.2.cloned.1.call-done) | data formatting | bytes 1048576
  (7 shorter events, 0.1 us)
Async XLA Ops:
  7.2 64.8 %copy-start = (f32[3072]{0:T(1024)S(1)}, f32[3072]{0:T(1024)}, u32[]{:S(2)}) copy-start(f32[3072]{0:T(1024)} %param.11) | copy-start | bytes 36868
  7.2 21.2 %copy-start.2 = (bf16[384,512]{1,0:T(8,128)(2,1)S(1)}, bf16[384,512]{1,0:T(8,128)(2,1)}, u32[]{:S(2)}) copy-start(bf16[384,512]{1,0:T(8,128)(2,1)} %param.7) | copy-start | bytes 1179652
  7.2 57.9 %all-gather.2.cloned.1.call-start = ((), (), s32[]{:S(2)}) async-start(), calls=%async_computation.1 | async-start | bytes 3932160 | tf_op jit(solution)/shard_map/all_gather | solution.py:65
  7.2 21.1 %collective-permute-start.1 = (bf16[384,512]{1,0:T(8,128)(2,1)}, bf16[384,512]{1,0:T(8,128)(2,1)S(1)}, u32[]{:S(2)}, u32[]{:S(2)}) collective-permute-start(bf16[384,512]{1,0:T(8,128)(2,1)} %param.7), channel_id=1, source_target_pairs={{0,4},{4,8},{8,12},{12,16},{16,20},{20,24},{24,28},{28,0},{1,5},{5... | collective-permute-start | bytes 1179656 | tf_op jit(solution)/shard_map/ppermute | solution.py:15
  10.3 19.2 %collective-permute-start.2 = (bf16[384,512]{1,0:T(8,128)(2,1)}, bf16[384,512]{1,0:T(8,128)(2,1)S(1)}, u32[]{:S(2)}, u32[]{:S(2)}) collective-permute-start(bf16[384,512]{1,0:T(8,128)(2,1)} %param.7), channel_id=1, source_target_pairs={{4,0},{8,4},{12,8},{16,12},{20,16},{24,20},{28,24},{0,28},{5,1},{9... | collective-permute-start | bytes 1179656 | tf_op jit(solution)/shard_map/ppermute | solution.py:18
  14.4 13.9 %collective-permute-start = (bf16[128,512]{1,0:T(8,128)(2,1)S(1)}, bf16[128,512]{1,0:T(8,128)(2,1)S(1)}, u32[]{:S(2)}, u32[]{:S(2)}) collective-permute-start(bf16[128,512]{1,0:T(8,128)(2,1)S(1)} %get-tuple-element.9), channel_id=1, source_target_pairs={{0,8},{4,12},{8,16},{12,20},{16,24},{20,28},{24,0},{28,4},{1,9},{5... | collective-permute-start | bytes 393224 | tf_op jit(solution)/shard_map/ppermute | solution.py:25
  14.4 15.1 %collective-permute-start.3 = (bf16[128,512]{1,0:T(8,128)(2,1)S(1)}, bf16[128,512]{1,0:T(8,128)(2,1)S(1)}, u32[]{:S(2)}, u32[]{:S(2)}) collective-permute-start(bf16[128,512]{1,0:T(8,128)(2,1)S(1)} %get-tuple-element.8), channel_id=1, source_target_pairs={{0,24},{4,28},{8,0},{12,4},{16,8},{20,12},{24,16},{28,20},{1,25},{... | collective-permute-start | bytes 393224 | tf_op jit(solution)/shard_map/ppermute | solution.py:25
  29.6 1.1 copy-start.1
  34.6 0.7 copy-start.4
  36.3 31.6 %copy-start.5 = (bf16[3,128,512]{2,1,0:T(8,128)(2,1)S(1)}, bf16[3,128,512]{2,1,0:T(8,128)(2,1)}, u32[]{:S(2)}) copy-start(bf16[3,128,512]{2,1,0:T(8,128)(2,1)} %copy-done.4) | copy-start | bytes 1179652
  36.3 123.4 %reduce-scatter.2.cloned.1.call-start = ((), (), s32[]{:S(2)}) async-start(), calls=%async_computation.2 | async-start | bytes 4718592 | tf_op jit(solution)/shard_map/reduce_scatter | solution.py:73
  65.1 2.9 %copy-start.3 = (bf16[2,384,2048]{2,1,0:T(8,128)(2,1)S(1)}, bf16[2,384,2048]{2,1,0:T(8,128)(2,1)}, u32[]{:S(2)}) copy-start(bf16[2,384,2048]{2,1,0:T(8,128)(2,1)} %all-gather.2.cloned.1.call-done) | copy-start | bytes 9437188
  71.2 0.7 copy-start.6
Sparse Core Ops, SparseCore 0:
  36.4 28.6 all-gather.1
  71.4 88.2 reduce-scatter.1
where the time goes:
time: 191 us
  waiting for transfers between devices  112 us (59%)
  local copies, waits for them, and re-layouts  21.3 us (11%)
  blocking collectives  20.1 us (11%)
  between operations  14.2 us (7%)
  starting transfers between devices  10.1 us (5%)
  matrix products  7.9 us (4%)
  other arithmetic  4.96 us (3%)
    reduce_scatter x1, waiting for transfers between devices, body(): lax.psum_scatter(partial_flux, 'atoms', scatter_dimension=1, tiled=True)  74.3 us
    all_gather x1, waiting for transfers between devices, body(): piece = lax.all_gather(stacked, 'modes', axis=2, tiled=True)  28.7 us
    psum x1, blocking collectives, body(): diffusivity = lax.psum(partial_sums, 'atoms') / mode_total  20.1 us
    gather x1, local copies, waits for them, and re-layouts, body(): frequency = spectrum[mode_index]  11.8 us
    ppermute x2, waiting for transfers between devices, from_behind(): lax.ppermute(value, axis, [(i, (i + by) % devices) for i in range(devices)])  8.03 us
    unnamed x19, local copies, waits for them, and re-layouts  4.68 us
    ppermute x2, starting transfers between devices, from_behind(): lax.ppermute(value, axis, [(i, (i + by) % devices) for i in range(devices)])  3.87 us
  transfers between devices with their start and end apart: 6, of which 4 were waited for; matrix products, arithmetic and copies ran while one was open for 9% of the time, Pallas kernels for 0%

commit v1 on v0

--- a/solution.py
+++ b/solution.py
@@ -76,7 +76,7 @@
     col_width = lax.dynamic_slice_in_dim(linewidth, atom_rank * share_cols, share_cols)
     weight = pair_weight(row_freq, col_freq, row_width, col_width)
     partial_sums = jnp.sum(weight * flux_tiles * flux_tiles, axis=1)
-    diffusivity = lax.psum(partial_sums, "atoms") / mode_total
+    diffusivity = jnp.sum(lax.all_gather(partial_sums, "atoms"), axis=0) / mode_total
     return (flux_tiles, diffusivity)
 
 

time: 191 us -> 197 us (1.031)
  blocking collectives: 20.1 us -> 26.1 us
    all_gather x0 -> x1, blocking collectives: none -> 26.1 us  [body(): lax.all_gather(partial_sums, 'atoms')]
    psum x1 -> x0, blocking collectives: 20.1 us -> none  [body(): diffusivity = lax.psum(partial_sums, 'atoms') / mode_total]
  transfers between devices with their start and end apart: 6 -> 6, of which waited for: 4 -> 4; matrix products, arithmetic and copies ran while one was open for 9% -> 8% of each run, Pallas kernels for 0% -> 0%
where the time goes in v1:
time: 197 us
  waiting for transfers between devices  112 us (57%)
  blocking collectives  26.1 us (13%)
  local copies, waits for them, and re-layouts  21.3 us (11%)
  between operations  14.2 us (7%)
  starting transfers between devices  10.1 us (5%)
  matrix products  7.9 us (4%)
  other arithmetic  4.98 us (3%)
    reduce_scatter x1, waiting for transfers between devices, body(): lax.psum_scatter(partial_flux, 'atoms', scatter_dimension=1, tiled=True)  74.3 us
    all_gather x1, waiting for transfers between devices, body(): piece = lax.all_gather(stacked, 'modes', axis=2, tiled=True)  28.7 us
    all_gather x1, blocking collectives, body(): lax.all_gather(partial_sums, 'atoms')  26.1 us
    gather x1, local copies, waits for them, and re-layouts, body(): frequency = spectrum[mode_index]  11.8 us
    ppermute x2, waiting for transfers between devices, from_behind(): lax.ppermute(value, axis, [(i, (i + by) % devices) for i in range(devices)])  8.03 us
    unnamed x19, local copies, waits for them, and re-layouts  4.68 us
  transfers between devices with their start and end apart: 6, of which 4 were waited for; matrix products, arithmetic and copies ran while one was open for 8% of the time, Pallas kernels for 0%

profile of v1, /device:TPU:0, one launch (start us, length us, event | category | flops | bytes accessed | tf_op | source)
XLA Modules:
  0.0 196.8 jit_solution(10073380010468895927)
XLA Ops:
  7.2 0.0 copy-start
  7.2 0.0 copy-start.2
  7.2 0.0 all-gather.4.cloned.1.call-start
  7.2 3.0 %collective-permute-start.1 = (bf16[384,512]{1,0:T(8,128)(2,1)}, bf16[384,512]{1,0:T(8,128)(2,1)S(1)}, u32[]{:S(2)}, u32[]{:S(2)}) collective-permute-start(bf16[384,512]{1,0:T(8,128)(2,1)} %param.7), channel_id=1, source_target_pairs={{0,4},{4,8},{8,12},{12,16},{16,20},{20,24},{24,28},{28,0},{1,5},{5... | collective-permute-start | bytes 1179656 | tf_op jit(solution)/shard_map/ppermute | solution.py:15
  10.3 3.1 %collective-permute-start.2 = (bf16[384,512]{1,0:T(8,128)(2,1)}, bf16[384,512]{1,0:T(8,128)(2,1)S(1)}, u32[]{:S(2)}, u32[]{:S(2)}) collective-permute-start(bf16[384,512]{1,0:T(8,128)(2,1)} %param.7), channel_id=1, source_target_pairs={{4,0},{8,4},{12,8},{16,12},{20,16},{24,20},{28,24},{0,28},{5,1},{9... | collective-permute-start | bytes 1179656 | tf_op jit(solution)/shard_map/ppermute | solution.py:18
  13.4 1.0 fusion.8
  14.4 0.1 collective-permute-start
  14.4 3.8 %collective-permute-start.3 = (bf16[128,512]{1,0:T(8,128)(2,1)S(1)}, bf16[128,512]{1,0:T(8,128)(2,1)S(1)}, u32[]{:S(2)}, u32[]{:S(2)}) collective-permute-start(bf16[128,512]{1,0:T(8,128)(2,1)S(1)} %get-tuple-element.10), channel_id=1, source_target_pairs={{0,24},{4,28},{8,0},{12,4},{16,8},{20,12},{24,16},{28,20},{1,25},{... | collective-permute-start | bytes 393224 | tf_op jit(solution)/shard_map/ppermute | solution.py:25
  18.3 0.7 compare_select_fusion.1
  19.0 1.2 broadcast_compare_fusion
  20.2 0.1 reshape.31
  20.2 8.0 %collective-permute-done = bf16[128,512]{1,0:T(8,128)(2,1)S(1)} collective-permute-done((bf16[128,512]{1,0:T(8,128)(2,1)S(1)}, bf16[128,512]{1,0:T(8,128)(2,1)S(1)}, u32[]{:S(2)}, u32[]{:S(2)}) %collective-permute-start) | collective-permute-done | bytes 131104 | tf_op jit(solution)/shard_map/ppermute | solution.py:25
  28.3 0.0 collective-permute-done.1
  28.3 0.0 copy-done.2
  28.4 1.1 collective-permute-done.2
  29.5 0.0 collective-permute-done.3
  29.6 0.0 copy-start.1
  29.6 1.1 copy-done.1
  30.7 2.1 %gather_fusion = bf16[24,128,512]{2,1,0:T(8,128)(2,1)S(1)} fusion(bf16[11,128,512]{2,1,0:T(8,128)(2,1)} %bitcast.23, s32[1024]{0:T(1024)S(1)} %pad_clamp_fusion), kind=kCustom, calls=%fused_computation | custom fusion | bytes 6291552 | tf_op jit(solution)/shard_map/gather | solution.py:57
  32.8 1.8 fusion.1
  34.6 0.0 copy-start.4
  34.6 0.7 copy-done.4
  35.3 1.0 pad_maximum_fusion
  36.3 0.0 all-gather.4.cloned.1.call-update
  36.3 0.0 copy-start.5
  36.3 0.0 reduce-scatter.2.cloned.1.call-start
  36.4 28.7 %all-gather.4.cloned.1.call-done = bf16[2,384,2048]{2,1,0:T(8,128)(2,1)} async-done(((bf16[2,384,512]{2,1,0:T(8,128)(2,1)}), bf16[2,384,2048]{2,1,0:T(8,128)(2,1)}) %all-gather.4.cloned.1.call-update) | async-done | bytes 3145744 | tf_op jit(solution)/shard_map/all_gather | solution.py:65
  65.1 0.0 copy-start.3
  65.1 2.9 %fusion = f32[2048,512]{1,0:T(8,128)S(1)} fusion(bf16[384,512]{1,0:T(8,128)(2,1)S(1)} %copy-done.2, bf16[2,384,2048]{2,1,0:T(8,128)(2,1)} %all-gather.4.cloned.1.call-done), kind=kOutput, calls=%fused_computation.5 | convolution fusion | flops 805306368 | bytes 6160384 | tf_op jit(solution)/shard_map/dot_general | solution.py:66
  68.0 0.0 copy-done.5
  68.0 0.0 copy-done.3
  68.0 3.3 %bitcast_subtract_fusion = f32[512,2048]{0,1:T(8,128)} fusion(f32[2048,512]{1,0:T(8,128)S(1)} %fusion, bf16[384,512]{1,0:T(8,128)(2,1)S(1)} %bitcast.26, bf16[2,384,2048]{2,1,0:T(8,128)(2,1)S(1)} %copy-done.3), kind=kOutput, calls=%fused_computation.2 | convolution fusion | flops 806354944 | bytes 10354688 | tf_op jit(solution)/shard_map/dot_general | solution.py:67
  71.2 0.0 copy-start.6
  71.2 0.0 reduce-scatter.2.cloned.1.call-update
  71.3 0.7 copy-done.6
  71.9 0.0 copy-done
  71.9 11.8 %gather_fusion.1 = f32[2048]{0:T(1024)S(1)} fusion(f32[3072]{0:T(1024)S(1)} %copy-done, s32[2048]{0:T(1024)S(1)} %fusion.6), kind=kCustom, calls=%fused_computation.1 | custom fusion | bytes 24576 | tf_op jit(solution)/shard_map/gather | solution.py:69
  83.7 0.1 dynamic_slice.13
  83.8 0.8 dynamic_slice.15
  84.6 0.8 dynamic_slice.14
  85.3 0.1 broadcast_multiply_fusion.1
  85.4 74.3 %reduce-scatter.2.cloned.1.call-done = f32[512,256]{0,1:T(8,128)} async-done(((f32[512,2048]{0,1:T(8,128)}), f32[512,256]{0,1:T(8,128)}) %reduce-scatter.2.cloned.1.call-update) | async-done | bytes 524304 | tf_op jit(solution)/shard_map/reduce_scatter | solution.py:73
  159.7 1.4 fusion.4
  161.2 26.1 %all-gather.1 = f32[8,1,512]{2,1,0:T(1,128)S(1)} all-gather(f32[1,1,512]{2,1,0:T(1,128)S(1)} %bitcast.27), channel_id=2, replica_groups=mesh['atoms'=8,'modes'=4] {'atoms'}, dimensions={0}, use_global_device_ids=true | all-gather | bytes 18432 | tf_op jit(solution)/shard_map/all_gather | solution.py:79
  187.3 0.6 broadcast_multiply_fusion
  187.9 2.0 %copy.14 = f32[512,256]{1,0:T(8,128)} copy(f32[512,256]{0,1:T(8,128)} %reduce-scatter.2.cloned.1.call-done) | data formatting | bytes 1048576
  (8 shorter events, 0.1 us)
Async XLA Ops:
  7.2 64.8 %copy-start = (f32[3072]{0:T(1024)S(1)}, f32[3072]{0:T(1024)}, u32[]{:S(2)}) copy-start(f32[3072]{0:T(1024)} %param.11) | copy-start | bytes 36868
  7.2 21.2 %copy-start.2 = (bf16[384,512]{1,0:T(8,128)(2,1)S(1)}, bf16[384,512]{1,0:T(8,128)(2,1)}, u32[]{:S(2)}) copy-start(bf16[384,512]{1,0:T(8,128)(2,1)} %param.7) | copy-start | bytes 1179652
  7.2 57.9 %all-gather.4.cloned.1.call-start = ((), (), s32[]{:S(2)}) async-start(), calls=%async_computation.1 | async-start | bytes 3932160 | tf_op jit(solution)/shard_map/all_gather | solution.py:65
  7.2 21.1 %collective-permute-start.1 = (bf16[384,512]{1,0:T(8,128)(2,1)}, bf16[384,512]{1,0:T(8,128)(2,1)S(1)}, u32[]{:S(2)}, u32[]{:S(2)}) collective-permute-start(bf16[384,512]{1,0:T(8,128)(2,1)} %param.7), channel_id=1, source_target_pairs={{0,4},{4,8},{8,12},{12,16},{16,20},{20,24},{24,28},{28,0},{1,5},{5... | collective-permute-start | bytes 1179656 | tf_op jit(solution)/shard_map/ppermute | solution.py:15
  10.3 19.2 %collective-permute-start.2 = (bf16[384,512]{1,0:T(8,128)(2,1)}, bf16[384,512]{1,0:T(8,128)(2,1)S(1)}, u32[]{:S(2)}, u32[]{:S(2)}) collective-permute-start(bf16[384,512]{1,0:T(8,128)(2,1)} %param.7), channel_id=1, source_target_pairs={{4,0},{8,4},{12,8},{16,12},{20,16},{24,20},{28,24},{0,28},{5,1},{9... | collective-permute-start | bytes 1179656 | tf_op jit(solution)/shard_map/ppermute | solution.py:18
  14.4 13.9 %collective-permute-start = (bf16[128,512]{1,0:T(8,128)(2,1)S(1)}, bf16[128,512]{1,0:T(8,128)(2,1)S(1)}, u32[]{:S(2)}, u32[]{:S(2)}) collective-permute-start(bf16[128,512]{1,0:T(8,128)(2,1)S(1)} %get-tuple-element.11), channel_id=1, source_target_pairs={{0,8},{4,12},{8,16},{12,20},{16,24},{20,28},{24,0},{28,4},{1,9},{5... | collective-permute-start | bytes 393224 | tf_op jit(solution)/shard_map/ppermute | solution.py:25
  14.4 15.1 %collective-permute-start.3 = (bf16[128,512]{1,0:T(8,128)(2,1)S(1)}, bf16[128,512]{1,0:T(8,128)(2,1)S(1)}, u32[]{:S(2)}, u32[]{:S(2)}) collective-permute-start(bf16[128,512]{1,0:T(8,128)(2,1)S(1)} %get-tuple-element.10), channel_id=1, source_target_pairs={{0,24},{4,28},{8,0},{12,4},{16,8},{20,12},{24,16},{28,20},{1,25},{... | collective-permute-start | bytes 393224 | tf_op jit(solution)/shard_map/ppermute | solution.py:25
  29.6 1.1 copy-start.1
  34.6 0.7 copy-start.4
  36.3 31.6 %copy-start.5 = (bf16[3,128,512]{2,1,0:T(8,128)(2,1)S(1)}, bf16[3,128,512]{2,1,0:T(8,128)(2,1)}, u32[]{:S(2)}) copy-start(bf16[3,128,512]{2,1,0:T(8,128)(2,1)} %copy-done.4) | copy-start | bytes 1179652
  36.3 123.4 %reduce-scatter.2.cloned.1.call-start = ((), (), s32[]{:S(2)}) async-start(), calls=%async_computation.2 | async-start | bytes 4718592 | tf_op jit(solution)/shard_map/reduce_scatter | solution.py:73
  65.1 2.9 %copy-start.3 = (bf16[2,384,2048]{2,1,0:T(8,128)(2,1)S(1)}, bf16[2,384,2048]{2,1,0:T(8,128)(2,1)}, u32[]{:S(2)}) copy-start(bf16[2,384,2048]{2,1,0:T(8,128)(2,1)} %all-gather.4.cloned.1.call-done) | copy-start | bytes 9437188
  71.2 0.7 copy-start.6
Sparse Core Ops, SparseCore 0:
  36.4 28.6 all-gather.3
  71.4 88.2 reduce-scatter.1
